TPU v7x, 32 devices: a whole 2x2x4 slice. The times are simulated.
32 devices in a mesh: orient: 8 (over z, y), dom: 4 (over x, core).
Axes of the slice: x: 2, y: 2, z: 4, core: 2. Of those that a mesh axis runs over, the one named last changes fastest.
Arguments:
- particles: bfloat16 [256, 8448], P(('dom', 'orient')), parts along dimension 0, may hold values from -12 to 12
- defocus: float32 [256], P(('dom', 'orient')), parts along dimension 0, may hold values from 10 to 60
- inv_noise: float32 [4224], replicated, may hold values from 0.5 to 2
- references: bfloat16 [13824, 8448], P(('dom', 'orient')), parts along dimension 0, may hold values from -0.25 to 0.25
- thresholds: int32 [256], P('dom'), parts along dimension 0, may hold values from 512 to 1023
- range_start: int32 [256], P('dom'), parts along dimension 0, may hold values from 0 to 3455
- range_len: int32 [256], P('dom'), parts along dimension 0, may hold values from 36 to 1727
Outputs:
- posterior: float32 [256, 3456], P('dom', 'orient'), parts along dimension 0
- cumulative: float32 [256, 3456], P('dom', 'orient'), parts along dimension 0
- log_evidence: float32 [256], P('dom'), parts along dimension 0
- kept_mass: float32 [256], P('dom'), parts along dimension 0
There are 4 independent parts, one for each index of `dom`. A program takes and returns all parts, laid end to end along the dimension named above; an argument that names none is the same for every part. Nothing has to cross between parts.
All inputs are finite; a program needn't handle non-finite values.
Results may differ from a plain program's by a relative error of at most 0.0004.
The roundings to bfloat16 on the way count: a program that leaves them out, or rounds other values in their place, can miss the bound.
Values may be sent and summed in bfloat16 or wider, within the bound.
A program may use at most 64 MiB of HBM per device.

v0:
```python
import math
import jax
import jax.numpy as jnp
from jax import lax
from jax.sharding import PartitionSpec as P


def ctf_table(defocus, coef):
    index = jnp.arange(coef, dtype=jnp.int32)
    row_pos = (index // 128).astype(jnp.float32)
    col_pos = (index % 128 - 64).astype(jnp.float32)
    freq = math.pi * (row_pos * row_pos + col_pos * col_pos) / 16384.0
    return -jnp.sin(defocus[:, None] * freq[None, :] + 0.07)


def on_device(particles, defocus, inv_noise, references, thresholds, range_start, range_len):
    coef = inv_noise.shape[0]
    feat = 2 * coef
    ori_dev = references.shape[0]
    ctf = ctf_table(defocus, coef)
    ctf_both = jnp.concatenate([ctf, ctf], axis=1)
    noise_both = jnp.concatenate([inv_noise, inv_noise])
    weighted = (particles.astype(jnp.float32) * ctf_both * noise_both[None, :]).astype(jnp.bfloat16)
    ctf_power = (ctf * ctf * inv_noise[None, :]).astype(jnp.bfloat16)
    packed = jnp.concatenate([weighted, ctf_power], axis=1)
    real_part = references[:, :coef].astype(jnp.float32)
    imag_part = references[:, coef:].astype(jnp.float32)
    power = (real_part * real_part + imag_part * imag_part).astype(jnp.bfloat16)
    dims = (((1,), (1,)), ((), ()))
    piece = lax.all_gather(packed, "orient", axis=0, tiled=True)
    cross = lax.dot_general(piece[:, :feat], references, dims, preferred_element_type=jnp.float32)
    energy = lax.dot_general(piece[:, feat:], power, dims, preferred_element_type=jnp.float32)
    scores = cross - 0.5 * energy
    local_top = jnp.max(scores, axis=1)
    local_sum = jnp.sum(jnp.exp(scores - local_top[:, None]), axis=1)
    all_tops, all_sums = (
        lax.all_gather(local_top[None, :], "orient", axis=0, tiled=True),
        lax.all_gather(local_sum[None, :], "orient", axis=0, tiled=True),
    )
    top_score = jnp.max(all_tops, axis=0)
    scaled = all_sums * jnp.exp(all_tops - top_score[None, :])
    total = jnp.sum(scaled, axis=0)
    ranks = jnp.arange(all_tops.shape[0], dtype=jnp.int32)
    earlier_rows = (ranks < lax.axis_index("orient"))[:, None]
    shifted = jnp.sum(jnp.where(earlier_rows, scaled, 0.0), axis=0)
    expon = jnp.exp(scores - top_score[:, None])
    posterior = expon / total[:, None]
    row_ids = lax.broadcasted_iota(jnp.int32, (ori_dev, ori_dev), 0)
    col_ids = lax.broadcasted_iota(jnp.int32, (ori_dev, ori_dev), 1)
    upper = (row_ids <= col_ids).astype(jnp.float32)
    running = jnp.dot(
        expon, upper, precision=lax.Precision.HIGHEST, preferred_element_type=jnp.float32
    )
    cumulative = (shifted[:, None] + running) / total[:, None]
    before = cumulative - posterior
    fraction = thresholds.astype(jnp.float32) / 1024.0
    kept = jnp.minimum(jnp.maximum(fraction[:, None] - before, 0.0), posterior)
    all_orients = lax.axis_size("orient") * ori_dev
    orient_ids = lax.axis_index("orient") * ori_dev + jnp.arange(ori_dev, dtype=jnp.int32)
    inside = (orient_ids[None, :] - range_start[:, None]) % all_orients < range_len[:, None]
    local_kept = jnp.sum(jnp.where(inside, kept, 0.0), axis=1)
    kept_mass = lax.psum(local_kept, "orient")
    log_evidence = top_score + jnp.log(total)
    return (posterior, cumulative, log_evidence, kept_mass)


def solution(mesh):
    return jax.shard_map(
        on_device,
        mesh=mesh,
        in_specs=(
            P(("dom", "orient"), None),
            P(("dom", "orient")),
            P(),
            P(("dom", "orient"), None),
            P("dom"),
            P("dom"),
            P("dom"),
        ),
        out_specs=(P("dom", "orient"), P("dom", "orient"), P("dom"), P("dom")),
        check_vma=False,
    )
```

profile of v0, /device:TPU:0, one launch (start us, length us, event | category | flops | bytes accessed | tf_op | source)
XLA Modules:
  0.0 113.0 jit_solution(12283271416409016182)
XLA Ops:
  7.2 0.0 all-gather.4.cloned.1.call-start
  7.2 0.8 pad_maximum_fusion.1
  8.0 1.3 %fusion.7 = (f32[8,4224]{1,0:T(8,128)S(1)}, bf16[8,4224]{1,0:T(8,128)(2,1)S(1)}) fusion(f32[4224]{0:T(1024)S(1)} %fusion.23, f32[8]{0:T(128)} %param.8, f32[4224]{0:T(1024)} %param.9), kind=kLoop, calls=%fused_computation.16 | loop fusion | flops 202752 | bytes 236576 | tf_op jit(solution)/shard_map/neg | solution.py:13
  9.3 1.0 fusion.6
  10.3 0.7 pad_maximum_fusion
  11.0 0.0 all-gather.4.cloned.1.call-update
  11.0 1.2 %dynamic-slice = u32[1]{0:T(128)} dynamic-slice(u32[32]{0:T(128)} %constant.75, u32[]{:T(128)S(6)} %add.76), dynamic_slice_sizes={1} | dynamic-slice | bytes 12
  12.9 0.7 convert_multiply_fusion
  13.6 45.1 %all-gather.4.cloned.1.call-done = bf16[64,12672]{1,0:T(8,128)(2,1)} async-done(((bf16[8,12672]{1,0:T(8,128)(2,1)}), bf16[64,12672]{1,0:T(8,128)(2,1)}) %all-gather.4.cloned.1.call-update) | async-done | bytes 1622032 | tf_op jit(solution)/shard_map/all_gather | solution.py:30
  58.6 0.0 copy-start
  58.7 0.0 copy-start.1
  58.7 5.0 %fusion.2 = f32[64,432]{1,0:T(8,128)S(1)} fusion(bf16[432,8448]{1,0:T(8,128)(2,1)} %param.10, bf16[64,12672]{1,0:T(8,128)(2,1)} %all-gather.4.cloned.1.call-done), kind=kOutput, calls=%fused_computation.5 | convolution fusion | flops 244546560 | bytes 7950336 | tf_op jit(solution)/shard_map/dot_general | solution.py:32
  63.6 0.4 copy-done
  64.0 0.4 copy-done.1
  64.4 0.0 copy-start.2
  64.4 0.0 copy-start.3
  64.5 2.3 %fusion.30 = (f32[64]{0:T(128)S(1)}, f32[64,432]{1,0:T(8,128)S(1)}) fusion(f32[64,432]{1,0:T(8,128)S(1)} %fusion.2, bf16[432,8448]{1,0:T(8,128)(2,1)S(1)} %copy-done, bf16[64,12672]{1,0:T(8,128)(2,1)S(1)} %copy-done.1), kind=kOutput, calls=%fused_computation.53 | convolution fusion | flops 467195840 | bytes 8622336 | tf_op jit(solution)/shard_map/dot_general | solution.py:31
  66.8 0.2 exponential_reduce_fusion
  67.0 0.2 dynamic-update-slice
  67.2 0.2 dynamic-update-slice.1
  67.4 18.8 %all-reduce.2 = (f32[512]{0:T(512)S(1)}, f32[512]{0:T(512)S(1)}) all-reduce(f32[512]{0:T(512)S(1)} %dynamic-update-slice.1, f32[512]{0:T(512)S(1)} %dynamic-update-slice), channel_id=3, replica_groups=mesh['orient'=8,'dom'=4] {'orient'}, use_global_device_ids=true, to_apply=%add.1 | all-reduce | flops 1024 | bytes 8192
  86.2 0.1 reshape.54
  86.3 0.1 reshape.55
  86.4 0.1 select_reduce_fusion.1
  86.4 0.5 log_add_fusion
  87.0 0.0 copy-done.2
  87.0 0.0 copy-done.3
  87.0 1.2 %select_reduce_fusion = (f32[64]{0:T(128)S(1)}, f32[64,432]{1,0:T(8,128)}, f32[64,432]{1,0:T(8,128)}) fusion(f32[64]{0:T(128)S(1)} %convert_multiply_fusion, s32[64]{0:T(128)S(1)} %copy-done.2, s32[64]{0:T(128)S(1)} %copy-done.3, s32[432]{0:T(512)S(1)} %iota_add_fusion, f32[64]{0:T(128)S(1)} %get-tuple-element.5, f32[64,432]{1,0:T(8,128)S(1)} %get-tuple-element.13, ...), kind=kOutput, calls=%fused_computation.18 | convolution fusion | flops 144039104 | bytes 335296 | tf_op jit(solution)/shard_map/dot_general | solution.py:51
  88.1 18.0 %psum.7 = f32[64]{0:T(128)} all-reduce(f32[64]{0:T(128)S(1)} %get-tuple-element.8), channel_id=1, replica_groups=mesh['orient'=8,'dom'=4] {'orient'}, use_global_device_ids=true, to_apply=%region_6.7 | all-reduce | flops 64 | bytes 512 | tf_op jit(solution)/shard_map/psum | solution.py:62
  (6 shorter events, 0.0 us)
Async XLA Ops:
  7.2 51.5 %all-gather.4.cloned.1.call-start = ((), (), s32[]{:S(2)}) async-start(), calls=%async_computation | async-start | bytes 1824768 | tf_op jit(solution)/shard_map/all_gather | solution.py:30
  58.6 5.4 %copy-start = (bf16[432,8448]{1,0:T(8,128)(2,1)S(1)}, bf16[432,8448]{1,0:T(8,128)(2,1)}, u32[]{:S(2)}) copy-start(bf16[432,8448]{1,0:T(8,128)(2,1)} %param.10) | copy-start | bytes 21897220
  58.7 5.8 %copy-start.1 = (bf16[64,12672]{1,0:T(8,128)(2,1)S(1)}, bf16[64,12672]{1,0:T(8,128)(2,1)}, u32[]{:S(2)}) copy-start(bf16[64,12672]{1,0:T(8,128)(2,1)} %all-gather.4.cloned.1.call-done) | copy-start | bytes 4866052
  64.4 22.5 %copy-start.2 = (s32[64]{0:T(128)S(1)}, s32[64]{0:T(128)}, u32[]{:S(2)}) copy-start(s32[64]{0:T(128)} %param.13) | copy-start | bytes 772
  64.4 22.5 %copy-start.3 = (s32[64]{0:T(128)S(1)}, s32[64]{0:T(128)}, u32[]{:S(2)}) copy-start(s32[64]{0:T(128)} %param.12) | copy-start | bytes 772
Sparse Core Ops, SparseCore 0:
  11.1 47.4 all-gather.3
where the time goes:
time: 113 us
  waiting for transfers between devices  45.1 us (40%)
  blocking collectives  36.7 us (32%)
  between operations  14.7 us (13%)
  matrix products  8.47 us (7%)
  other arithmetic  5.25 us (5%)
  local copies, waits for them, and re-layouts  2.66 us (2%)
    all_gather x1, waiting for transfers between devices, on_device(): piece = lax.all_gather(packed, 'orient', axis=0, tiled=True)  45.1 us
    unnamed x1, blocking collectives  18.8 us
    psum x1, blocking collectives, on_device(): kept_mass = lax.psum(local_kept, 'orient')  18 us
    dot_general x1, matrix products, on_device(): lax.dot_general(piece[:, feat:], power, dims, preferred_element_type=jnp....  4.98 us
    unnamed x13, local copies, waits for them, and re-layouts  2.51 us
    dot_general x1, matrix products, on_device(): lax.dot_general(piece[:, :feat], references, dims, preferred_element_type...  2.33 us
  transfers between devices with their start and end apart: 1, of which 1 were waited for; matrix products, arithmetic and copies ran while one was open for 2% of the time, Pallas kernels for 0%

commit v1 on v0

--- a/solution.py
+++ b/solution.py
@@ -59,7 +59,11 @@
     orient_ids = lax.axis_index("orient") * ori_dev + jnp.arange(ori_dev, dtype=jnp.int32)
     inside = (orient_ids[None, :] - range_start[:, None]) % all_orients < range_len[:, None]
     local_kept = jnp.sum(jnp.where(inside, kept, 0.0), axis=1)
-    kept_mass = lax.psum(local_kept, "orient")
+    kept_mass = local_kept
+    for hop in (1, 2, 4):
+        kept_mass = kept_mass + lax.ppermute(
+            kept_mass, "orient", [(dev, dev ^ hop) for dev in range(8)]
+        )
     log_evidence = top_score + jnp.log(total)
     return (posterior, cumulative, log_evidence, kept_mass)
 

time: 113 us -> 107 us (0.947)
  blocking collectives: 36.7 us -> 18.8 us
  waiting for transfers between devices: 45.1 us -> 55.8 us
    psum x1 -> x0, blocking collectives: 18 us -> none  [on_device(): kept_mass = lax.psum(local_kept, 'orient')]
    ppermute x0 -> x3, waiting for transfers between devices: none -> 10.7 us  [on_device(): lax.ppermute(kept_mass, 'orient', [(dev, dev ^ hop) for dev in range(8)])]
  transfers between devices with their start and end apart: 1 -> 4, of which waited for: 1 -> 4; matrix products, arithmetic and copies ran while one was open for 2% -> 2% of each run, Pallas kernels for 0% -> 0%
where the time goes in v1:
time: 107 us
  waiting for transfers between devices  55.8 us (52%)
  blocking collectives  18.8 us (18%)
  between operations  14.8 us (14%)
  matrix products  8.47 us (8%)
  other arithmetic  5.77 us (5%)
  local copies, waits for them, and re-layouts  2.66 us (2%)
    all_gather x1, waiting for transfers between devices, on_device(): piece = lax.all_gather(packed, 'orient', axis=0, tiled=True)  45.1 us
    unnamed x1, blocking collectives  18.8 us
    ppermute x3, waiting for transfers between devices, on_device(): lax.ppermute(kept_mass, 'orient', [(dev, dev ^ hop) for dev in range(8)])  10.7 us
    dot_general x1, matrix products, on_device(): lax.dot_general(piece[:, feat:], power, dims, preferred_element_type=jnp....  4.98 us
    unnamed x13, local copies, waits for them, and re-layouts  2.51 us
    dot_general x1, matrix products, on_device(): lax.dot_general(piece[:, :feat], references, dims, preferred_element_type...  2.33 us
  transfers between devices with their start and end apart: 4, of which 4 were waited for; matrix products, arithmetic and copies ran while one was open for 2% of the time, Pallas kernels for 0%

profile of v1, /device:TPU:0, one launch (start us, length us, event | category | flops | bytes accessed | tf_op | source)
XLA Modules:
  0.0 106.7 jit_solution(2375181934518018125)
XLA Ops:
  7.2 0.0 all-gather.4.cloned.1.call-start
  7.2 0.8 pad_maximum_fusion.1
  8.0 1.3 %fusion.7 = (f32[8,4224]{1,0:T(8,128)S(1)}, bf16[8,4224]{1,0:T(8,128)(2,1)S(1)}) fusion(f32[4224]{0:T(1024)S(1)} %fusion.23, f32[8]{0:T(128)} %param.8, f32[4224]{0:T(1024)} %param.9), kind=kLoop, calls=%fused_computation.16 | loop fusion | flops 202752 | bytes 236576 | tf_op jit(solution)/shard_map/neg | solution.py:13
  9.3 1.0 fusion.6
  10.3 0.7 pad_maximum_fusion
  11.0 0.0 all-gather.4.cloned.1.call-update
  11.0 1.2 %dynamic-slice = u32[1]{0:T(128)} dynamic-slice(u32[32]{0:T(128)} %constant.75, u32[]{:T(128)S(6)} %add.86), dynamic_slice_sizes={1} | dynamic-slice | bytes 12
  12.9 0.7 convert_multiply_fusion
  13.6 45.1 %all-gather.4.cloned.1.call-done = bf16[64,12672]{1,0:T(8,128)(2,1)} async-done(((bf16[8,12672]{1,0:T(8,128)(2,1)}), bf16[64,12672]{1,0:T(8,128)(2,1)}) %all-gather.4.cloned.1.call-update) | async-done | bytes 1622032 | tf_op jit(solution)/shard_map/all_gather | solution.py:30
  58.6 0.0 copy-start
  58.7 5.0 %fusion.2 = f32[64,432]{1,0:T(8,128)S(1)} fusion(bf16[432,8448]{1,0:T(8,128)(2,1)} %param.10, bf16[64,12672]{1,0:T(8,128)(2,1)} %all-gather.4.cloned.1.call-done), kind=kOutput, calls=%fused_computation.5 | convolution fusion | flops 244546560 | bytes 7950336 | tf_op jit(solution)/shard_map/dot_general | solution.py:32
  63.6 0.4 copy-done
  64.0 0.4 copy-done.1
  64.5 2.3 %fusion.30 = (f32[64]{0:T(128)S(1)}, f32[64,432]{1,0:T(8,128)S(1)}) fusion(f32[64,432]{1,0:T(8,128)S(1)} %fusion.2, bf16[432,8448]{1,0:T(8,128)(2,1)S(1)} %copy-done, bf16[64,12672]{1,0:T(8,128)(2,1)S(1)} %copy-done.1), kind=kOutput, calls=%fused_computation.53 | convolution fusion | flops 467195840 | bytes 8622336 | tf_op jit(solution)/shard_map/dot_general | solution.py:31
  66.8 0.2 exponential_reduce_fusion
  67.0 0.2 dynamic-update-slice
  67.2 0.2 dynamic-update-slice.1
  67.4 18.8 %all-reduce.2 = (f32[512]{0:T(512)S(1)}, f32[512]{0:T(512)S(1)}) all-reduce(f32[512]{0:T(512)S(1)} %dynamic-update-slice.1, f32[512]{0:T(512)S(1)} %dynamic-update-slice), channel_id=3, replica_groups=mesh['orient'=8,'dom'=4] {'orient'}, use_global_device_ids=true, to_apply=%add.1 | all-reduce | flops 1024 | bytes 8192
  86.2 0.1 reshape.54
  86.3 0.1 reshape.55
  86.4 0.1 select_reduce_fusion.1
  86.4 0.0 copy-done.2
  86.5 0.0 copy-done.3
  86.5 1.2 %select_reduce_fusion = (f32[64]{0:T(128)S(1)}, f32[64,432]{1,0:T(8,128)}, f32[64,432]{1,0:T(8,128)}) fusion(f32[64]{0:T(128)S(1)} %convert_multiply_fusion, s32[64]{0:T(128)S(1)} %copy-done.2, s32[64]{0:T(128)S(1)} %copy-done.3, s32[432]{0:T(512)S(1)} %iota_add_fusion, f32[64]{0:T(128)S(1)} %get-tuple-element.5, f32[64,432]{1,0:T(8,128)S(1)} %get-tuple-element.13, ...), kind=kOutput, calls=%fused_computation.18 | convolution fusion | flops 144039104 | bytes 335296 | tf_op jit(solution)/shard_map/dot_general | solution.py:51
  87.6 0.4 collective-permute-start
  88.1 3.2 %collective-permute-done = f32[64]{0:T(128)S(1)} collective-permute-done((f32[64]{0:T(128)S(1)}, f32[64]{0:T(128)S(1)}, u32[]{:S(2)}, u32[]{:S(2)}) %collective-permute-start) | collective-permute-done | bytes 288 | tf_op jit(solution)/shard_map/ppermute | solution.py:64
  91.3 0.0 collective-permute-start.1
  91.3 3.6 %collective-permute-done.1 = f32[64]{0:T(128)S(1)} collective-permute-done((f32[64]{0:T(128)S(1)}, f32[64]{0:T(128)S(1)}, u32[]{:S(2)}, u32[]{:S(2)}) %collective-permute-start.1) | collective-permute-done | bytes 288 | tf_op jit(solution)/shard_map/ppermute | solution.py:64
  94.8 0.0 collective-permute-start.2
  94.8 0.5 log_add_fusion
  95.4 3.9 %collective-permute-done.2 = f32[64]{0:T(128)S(1)} collective-permute-done((f32[64]{0:T(128)S(1)}, f32[64]{0:T(128)S(1)}, u32[]{:S(2)}, u32[]{:S(2)}) %collective-permute-start.2) | collective-permute-done | bytes 288 | tf_op jit(solution)/shard_map/ppermute | solution.py:64
  99.3 0.5 add.85
  (11 shorter events, 0.1 us)
Async XLA Ops:
  7.2 51.5 %all-gather.4.cloned.1.call-start = ((), (), s32[]{:S(2)}) async-start(), calls=%async_computation | async-start | bytes 1824768 | tf_op jit(solution)/shard_map/all_gather | solution.py:30
  58.6 5.4 %copy-start = (bf16[432,8448]{1,0:T(8,128)(2,1)S(1)}, bf16[432,8448]{1,0:T(8,128)(2,1)}, u32[]{:S(2)}) copy-start(bf16[432,8448]{1,0:T(8,128)(2,1)} %param.10) | copy-start | bytes 21897220
  58.7 5.8 %copy-start.1 = (bf16[64,12672]{1,0:T(8,128)(2,1)S(1)}, bf16[64,12672]{1,0:T(8,128)(2,1)}, u32[]{:S(2)}) copy-start(bf16[64,12672]{1,0:T(8,128)(2,1)} %all-gather.4.cloned.1.call-done) | copy-start | bytes 4866052
  64.4 22.0 %copy-start.2 = (s32[64]{0:T(128)S(1)}, s32[64]{0:T(128)}, u32[]{:S(2)}) copy-start(s32[64]{0:T(128)} %param.13) | copy-start | bytes 772
  64.4 22.0 %copy-start.3 = (s32[64]{0:T(128)S(1)}, s32[64]{0:T(128)}, u32[]{:S(2)}) copy-start(s32[64]{0:T(128)} %param.12) | copy-start | bytes 772
  87.6 3.6 %collective-permute-start = (f32[64]{0:T(128)S(1)}, f32[64]{0:T(128)S(1)}, u32[]{:S(2)}, u32[]{:S(2)}) collective-permute-start(f32[64]{0:T(128)S(1)} %get-tuple-element.8), channel_id=1, source_target_pairs={{0,4},{4,0},{8,12},{12,8},{16,20},{20,16},{24,28},{28,24},{1,5},{5... | collective-permute-start | bytes 776 | tf_op jit(solution)/shard_map/ppermute | solution.py:64
  91.3 3.6 %collective-permute-start.1 = (f32[64]{0:T(128)S(1)}, f32[64]{0:T(128)S(1)}, u32[]{:S(2)}, u32[]{:S(2)}) collective-permute-start(f32[64]{0:T(128)S(1)} %add.83), channel_id=1, source_target_pairs={{0,8},{4,12},{8,0},{12,4},{16,24},{20,28},{24,16},{28,20},{1,9},{5... | collective-permute-start | bytes 776 | tf_op jit(solution)/shard_map/ppermute | solution.py:64
  94.8 4.5 %collective-permute-start.2 = (f32[64]{0:T(128)S(1)}, f32[64]{0:T(128)S(1)}, u32[]{:S(2)}, u32[]{:S(2)}) collective-permute-start(f32[64]{0:T(128)S(1)} %add.84), channel_id=1, source_target_pairs={{0,16},{4,20},{8,24},{12,28},{16,0},{20,4},{24,8},{28,12},{1,17},{... | collective-permute-start | bytes 776 | tf_op jit(solution)/shard_map/ppermute | solution.py:64
Sparse Core Ops, SparseCore 0:
  11.1 47.4 all-gather.3
